TPU v7x, 256 devices: a whole 4x4x8 slice. The times are simulated.
256 devices in a mesh: band: 16 (over y_lo, x, core), grid: 16 (over y_hi, z).
Axes of the slice: x: 4, y: 4 (y_hi: 2, y_lo: 2; y = y_hi * 2 + y_lo), z: 8, core: 2. Of those that a mesh axis runs over, the one named last changes fastest.
Arguments:
- orbitals: float32 [64, 48, 2304], P('band', 'grid'), may hold values from -5.5 to 6.6
- occupation: int32 [64], P('band'), may hold values from 0 to 2
- cutoff: int32 [], replicated, may hold values from 144 to 1728
Outputs:
- exchange_term: float32 [64, 48, 2304], P('band', 'grid')
All inputs are finite; a program needn't handle non-finite values.
Results may differ from a plain program's by a relative error of at most 0.00005.
Values sent between devices are 32-bit elements; how exact they have to be, the bound alone decides.
No kernel may reach another device: no remote copies, remote signals or barrier semaphores. Data moves between devices by JAX's collectives and lax.ppermute only.
A program may use at most 128 MiB of HBM per device.

v0:
```python
import jax
import jax.numpy as jnp
from jax import lax
from jax.sharding import PartitionSpec as P

G = 48
screen_alpha = 2.0
screen_scale = 4.0


def shifted(block, axis, distance):
    devices = range(lax.axis_size(axis))
    route = [((i - distance) % len(devices), i) for i in devices]
    return lax.ppermute(block, axis, route)


def transform_tables(extent, cutoff):
    position = jnp.arange(extent, dtype=jnp.int32)
    middle = extent // 2
    frequency = jnp.where(position <= middle, position, position - middle)
    phase_index = frequency[:, None] * position[None, :] % extent
    angles = 2.0 * jnp.pi / extent * phase_index.astype(jnp.float32)
    transform = jnp.where((position <= middle)[:, None], jnp.cos(angles), jnp.sin(angles))
    weight = jnp.where((position == 0) | (position == middle), 1.0, 2.0).astype(jnp.float32)
    shells = (
        frequency[:, None, None] ** 2
        + frequency[None, :, None] ** 2
        + frequency[None, None, :] ** 2
    )
    ratios = shells.astype(jnp.float32) / screen_alpha
    screen = jnp.where(
        shells > 0, (1.0 - jnp.exp(-ratios)) / jnp.maximum(ratios, 1.0 / screen_alpha), 1.0
    )
    factor = weight[:, None, None] * weight[None, :, None] * weight[None, None, :]
    kernel = jnp.where(shells <= cutoff, screen_scale * screen * factor / float(extent**3), 0.0)
    return (transform, kernel.reshape(extent, extent * extent))


def apply_transform(matrix, fields):
    batch_size, extent, row_cells = fields.shape
    first = jnp.matmul(matrix, fields, precision=lax.Precision.HIGHEST)
    second = jnp.matmul(
        matrix, first.reshape(batch_size * extent, extent, extent), precision=lax.Precision.HIGHEST
    )
    third = jnp.matmul(
        second.reshape(batch_size * extent * extent, extent),
        matrix.T,
        precision=lax.Precision.HIGHEST,
    )
    return third.reshape(batch_size, extent, row_cells)


def screened_potential(fields, transform, kernel):
    spectrum = apply_transform(transform, fields) * kernel[None]
    return apply_transform(transform.T, spectrum)


def solve_pairs(densities, transform, kernel):
    groups = lax.axis_size("grid")
    pair_count, planes, row_cells = densities.shape
    shaped = densities.reshape(groups, pair_count // groups, planes, row_cells)
    pieces = lax.all_to_all(shaped, "grid", split_axis=0, concat_axis=2, tiled=True)
    fields = pieces.reshape(pieces.shape[1], pieces.shape[2], pieces.shape[3])
    potential = screened_potential(fields, transform, kernel).reshape(pieces.shape)
    sliced = lax.all_to_all(potential, "grid", split_axis=2, concat_axis=0, tiled=True)
    return sliced.reshape(pair_count, planes, row_cells)


def pair_densities(home_orbitals, visitor_orbitals):
    orbital_count, planes, row_cells = home_orbitals.shape
    products = home_orbitals[:, None] * visitor_orbitals[None, :]
    return products.reshape(orbital_count * orbital_count, planes, row_cells)


def pair_terms(home_orbitals, home_weights, visitor_orbitals, visitor_weights, potentials):
    orbital_count, planes, row_cells = home_orbitals.shape
    shaped = potentials.reshape(orbital_count, orbital_count, planes, row_cells)
    scaled_visitor = visitor_weights[:, None, None] * visitor_orbitals
    scaled_home = home_weights[:, None, None] * home_orbitals
    to_home = jnp.sum(scaled_visitor[None] * shaped, axis=1)
    to_visitor = jnp.sum(scaled_home[:, None] * shaped, axis=0)
    return (to_home, to_visitor)


def on_device(orbitals, occupation, cutoff):
    transform, kernel = transform_tables(G, cutoff)
    weights = occupation.astype(jnp.float32) * 0.5
    half_cycle = lax.axis_size("band") // 2
    blocks = [(orbitals, weights)]
    visitor = (orbitals, weights)
    for distance in range(1, half_cycle + 1):
        visitor = shifted((orbitals, weights), "band", distance)
        blocks.append(visitor)
    densities = jnp.concatenate([pair_densities(orbitals, member[0]) for member in blocks], axis=0)
    potentials = solve_pairs(densities, transform, kernel)
    per_set = potentials.reshape(half_cycle + 1, -1, potentials.shape[1], potentials.shape[2])
    applied = jnp.zeros_like(orbitals)
    for distance in range(half_cycle + 1):
        member = blocks[distance]
        to_home, to_visitor = pair_terms(orbitals, weights, member[0], member[1], per_set[distance])
        applied = applied + to_home
        if 0 < distance < half_cycle:
            applied = applied + shifted(to_visitor, "band", -distance)
    return -applied


def solution(mesh):
    placed = (P("band", "grid", None), P("band"), P())
    return jax.shard_map(
        on_device, mesh=mesh, in_specs=placed, out_specs=P("band", "grid", None), check_vma=False
    )
```

profile of v0, /device:TPU:7, one launch (start us, length us, event | category | flops | bytes accessed | tf_op | source)
XLA Modules:
  0.0 483.2 jit_solution(18098811238183727219)
XLA Ops:
  0.0 1.8 collective-permute-start
  1.8 1.2 collective-permute-start.1
  3.0 1.2 collective-permute-start.2
  4.2 2.4 collective-permute-start.3
  6.6 1.7 collective-permute-start.5
  8.3 1.2 collective-permute-start.6
  11.3 2.4 collective-permute-done.4
  13.7 2.9 collective-permute-done.5
  17.2 1.2 broadcast_multiply_fusion
  19.7 2.3 copy-done
  22.0 10.4 %all-to-all-start = ((f32[16,9,3,2304]{3,2,1,0:T(4,128)}), f32[16,9,3,2304]{3,2,1,0:T(4,128)}, u32[]{:S(2)}, u32[]{:S(2)}) async-start(f32[16,9,3,2304]{3,2,1,0:T(4,128)} %bitcast.56), calls=%async_computation | async-start | bytes 10616832 | tf_op jit(solution)/shard_map/all_to_all | solution.py:62
  35.5 118.0 %all-to-all-done = f32[16,9,3,2304]{3,2,1,0:T(4,128)} async-done(((f32[16,9,3,2304]{3,2,1,0:T(4,128)}), f32[16,9,3,2304]{3,2,1,0:T(4,128)}, u32[]{:S(2)}, u32[]{:S(2)}) %all-to-all-start) | async-done | bytes 3981344 | tf_op jit(solution)/shard_map/all_to_all | solution.py:62
  153.5 5.9 %copy.131 = f32[1,9,16,3,2304]{4,3,2,1,0:T(4,128)} copy(f32[1,9,16,3,2304]{4,3,1,2,0:T(4,128)} %bitcast.14) | data formatting | bytes 7962624 | tf_op jit(solution)/shard_map/all_to_all | solution.py:62
  159.4 6.7 %reshape.334 = f32[9,48,2304]{2,1,0:T(8,128)} reshape(f32[1,9,16,3,2304]{4,3,2,1,0:T(4,128)} %copy.131) | data formatting | bytes 7962624 | tf_op jit(solution)/shard_map/reshape | solution.py:63
  166.2 7.7 %convolution_bitcast_fusion.1 = f32[9,48,2304]{2,1,0:T(8,128)} fusion(f32[9,48,2304]{2,1,0:T(8,128)} %reshape.334, s32[48]{0:T(128)S(1)} %add_select_fusion.1, pred[48]{0:T(512)(128)(4,1)S(1)} %iota_compare_fusion), kind=kOutput, calls=%fused_computation.1 | convolution fusion | flops 573331968 | bytes 7962864 | tf_op jit(solution)/shard_map/dot_general | solution.py:41
  173.9 10.3 %reshape.335 = f32[432,48,48]{2,1,0:T(8,128)} reshape(f32[9,48,2304]{2,1,0:T(8,128)} %convolution_bitcast_fusion.1) | data formatting | bytes 7962624 | tf_op jit(solution)/shard_map/reshape | solution.py:43
  184.2 9.5 %copy.134 = f32[432,48,48]{0,1,2:T(8,128)} copy(f32[432,48,48]{2,1,0:T(8,128)} %reshape.335) | data formatting | bytes 7962624 | tf_op jit(solution)/shard_map/reshape | solution.py:43
  193.6 7.6 %convolution_bitcast_fusion.3 = f32[432,48,48]{0,1,2:T(8,128)} fusion(f32[432,48,48]{0,1,2:T(8,128)} %copy.134, s32[48]{0:T(128)S(1)} %add_select_fusion.1, pred[48]{0:T(512)(128)(4,1)S(1)} %iota_compare_fusion), kind=kOutput, calls=%fused_computation.4 | convolution fusion | flops 573331968 | bytes 7962864 | tf_op jit(solution)/shard_map/dot_general | solution.py:42
  201.3 8.5 %copy.135 = f32[432,48,48]{1,0,2:T(8,128)} copy(f32[432,48,48]{0,1,2:T(8,128)} %convolution_bitcast_fusion.3) | data formatting | bytes 7962624 | tf_op jit(solution)/shard_map/transpose | solution.py:42
  209.7 9.3 %reshape.336 = f32[20736,48]{0,1:T(8,128)} reshape(f32[432,48,48]{1,0,2:T(8,128)} %copy.135) | data formatting | bytes 7962624 | tf_op jit(solution)/shard_map/reshape | solution.py:46
  219.0 20.2 %fusion.11 = f32[20736,48]{1,0:T(8,128)} fusion(f32[20736,48]{0,1:T(8,128)} %reshape.336, s32[48]{0:T(128)S(1)} %add_select_fusion.1, pred[48]{0:T(512)(128)(4,1)S(1)} %iota_compare_fusion), kind=kOutput, calls=%fused_computation.65 | convolution fusion | flops 573331968 | bytes 7962864 | tf_op jit(solution)/shard_map/dot_general | solution.py:45
  239.2 9.5 %reshape.337 = f32[9,48,2304]{2,1,0:T(8,128)} reshape(f32[20736,48]{1,0:T(8,128)} %fusion.11) | data formatting | bytes 7962624 | tf_op jit(solution)/shard_map/reshape | solution.py:50
  248.7 7.7 %convolution_bitcast_fusion = f32[9,48,2304]{2,1,0:T(8,128)} fusion(f32[9,48,2304]{2,1,0:T(8,128)} %reshape.337, f32[48,2304]{1,0:T(8,128)S(1)} %multiply_select_fusion, s32[48]{0:T(128)S(1)} %add_select_fusion.1, pred[48]{0:T(512)(128)(4,1)S(1)} %iota_compare_fusion), kind=kOutput, calls=%fused_computation | convolution fusion | flops 574327296 | bytes 8405232 | tf_op jit(solution)/shard_map/dot_general | solution.py:41
  256.4 10.7 %reshape.338 = f32[432,48,48]{2,1,0:T(8,128)} reshape(f32[9,48,2304]{2,1,0:T(8,128)} %convolution_bitcast_fusion) | data formatting | bytes 7962624 | tf_op jit(solution)/shard_map/reshape | solution.py:43
  267.1 9.5 %copy.137 = f32[432,48,48]{0,1,2:T(8,128)} copy(f32[432,48,48]{2,1,0:T(8,128)} %reshape.338) | data formatting | bytes 7962624 | tf_op jit(solution)/shard_map/reshape | solution.py:43
  276.5 8.6 %convolution_bitcast_fusion.2 = f32[432,48,48]{0,1,2:T(8,128)} fusion(f32[432,48,48]{0,1,2:T(8,128)} %copy.137, s32[48]{0:T(128)S(1)} %add_select_fusion.1, pred[48]{0:T(512)(128)(4,1)S(1)} %iota_compare_fusion), kind=kOutput, calls=%fused_computation.3 | convolution fusion | flops 573331968 | bytes 7962864 | tf_op jit(solution)/shard_map/dot_general | solution.py:42
  285.2 8.5 %copy.138 = f32[432,48,48]{1,0,2:T(8,128)} copy(f32[432,48,48]{0,1,2:T(8,128)} %convolution_bitcast_fusion.2) | data formatting | bytes 7962624 | tf_op jit(solution)/shard_map/transpose | solution.py:42
  293.6 9.1 %reshape.339 = f32[20736,48]{0,1:T(8,128)} reshape(f32[432,48,48]{1,0,2:T(8,128)} %copy.138) | data formatting | bytes 7962624 | tf_op jit(solution)/shard_map/reshape | solution.py:46
  302.7 20.3 %fusion.12 = f32[20736,48]{1,0:T(8,128)} fusion(f32[20736,48]{0,1:T(8,128)} %reshape.339, s32[48]{0:T(128)S(1)} %add_select_fusion.1, pred[48]{0:T(512)(128)(4,1)S(1)} %iota_compare_fusion), kind=kOutput, calls=%fused_computation.66 | convolution fusion | flops 573331968 | bytes 7962864 | tf_op jit(solution)/shard_map/dot_general | solution.py:45
  323.1 9.5 %reshape_reshape.6 = f32[1,9,48,2304]{3,2,1,0:T(8,128)} reshape(f32[20736,48]{1,0:T(8,128)} %fusion.12) | data formatting | bytes 7962624 | tf_op jit(solution)/shard_map/reshape;reshape | solution.py:64
  332.6 8.1 %copy.140 = f32[1,9,48,2304]{3,0,1,2:T(1,128)} copy(f32[1,9,48,2304]{3,2,1,0:T(8,128)} %reshape_reshape.6) | data formatting | bytes 7962624 | tf_op jit(solution)/shard_map/reshape;reshape | solution.py:64
  340.7 10.1 %all-to-all-start.1 = ((f32[1,9,48,2304]{3,0,1,2:T(1,128)}), f32[1,9,48,2304]{3,0,1,2:T(1,128)}, u32[]{:S(2)}, u32[]{:S(2)}) async-start(f32[1,9,48,2304]{3,0,1,2:T(1,128)} %copy.140), calls=%async_computation.1 | async-start | bytes 7962624 | tf_op jit(solution)/shard_map/all_to_all | solution.py:65
  350.8 7.1 %collective-permute-start.8 = (f32[4]{0:T(128)S(1)}, f32[4]{0:T(128)S(1)}, u32[]{:S(2)}, u32[]{:S(2)}) collective-permute-start(f32[4]{0:T(128)S(1)} %convert_multiply_fusion), channel_id=1, source_target_pairs={{240,0},{0,16},{16,32},{32,48},{48,64},{64,80},{80,96},{96,112},{1... | collective-permute-start | bytes 56 | tf_op jit(solution)/shard_map/ppermute | solution.py:14
  357.9 4.4 collective-permute-start.14
  362.7 2.9 collective-permute-start.20
  366.2 1.0 collective-permute-done.16
  368.0 74.5 %all-to-all-done.1 = f32[1,9,48,2304]{3,0,1,2:T(1,128)} async-done(((f32[1,9,48,2304]{3,0,1,2:T(1,128)}), f32[1,9,48,2304]{3,0,1,2:T(1,128)}, u32[]{:S(2)}, u32[]{:S(2)}) %all-to-all-start.1) | async-done | bytes 3981344 | tf_op jit(solution)/shard_map/all_to_all | solution.py:65
  442.5 5.3 %copy.141 = f32[1,9,48,2304]{3,0,2,1:T(1,128)S(1)} copy(f32[1,9,48,2304]{3,0,1,2:T(1,128)} %all-to-all-done.1) | data formatting | bytes 7962624 | tf_op jit(solution)/shard_map/all_to_all | solution.py:65
  447.8 1.4 copy.142
  449.2 1.1 fusion.32
  450.3 2.9 multiply_reduce_fusion.14
  453.3 4.9 %collective-permute-start.13 = (f32[4,3,2304]{2,1,0:T(4,128)S(1)}, f32[4,3,2304]{2,1,0:T(4,128)S(1)}, u32[]{:S(2)}, u32[]{:S(2)}) collective-permute-start(f32[4,3,2304]{2,1,0:T(4,128)S(1)} %get-tuple-element.29), channel_id=1, source_target_pairs={{48,0},{64,16},{80,32},{96,48},{112,64},{128,80},{144,96},{160,112... | collective-permute-start | bytes 331784 | tf_op jit(solution)/shard_map/ppermute | solution.py:14
  458.3 4.0 collective-permute-start.15
  462.8 1.7 collective-permute-start.19
  464.5 3.0 collective-permute-start.21
  467.5 4.1 collective-permute-done.13
  471.8 5.5 %collective-permute-done.19 = f32[4,3,2304]{2,1,0:T(4,128)S(1)} collective-permute-done((f32[4,3,2304]{2,1,0:T(4,128)S(1)}, f32[4,3,2304]{2,1,0:T(4,128)S(1)}, u32[]{:S(2)}, u32[]{:S(2)}) %collective-permute-start.19) | collective-permute-done | bytes 110624 | tf_op jit(solution)/shard_map/ppermute | solution.py:14
  477.3 4.5 collective-permute-done.21
  (87 shorter events, 9.2 us)
Async XLA Ops:
  0.0 6.6 %collective-permute-start = (f32[4,3,2304]{2,0,1:T(4,128)}, f32[4,3,2304]{2,0,1:T(4,128)S(1)}, u32[]{:S(2)}, u32[]{:S(2)}) collective-permute-start(f32[4,3,2304]{2,0,1:T(4,128)} %param.3), channel_id=1, source_target_pairs={{240,0},{0,16},{16,32},{32,48},{48,64},{64,80},{80,96},{96,112},{1... | collective-permute-start | bytes 331784 | tf_op jit(solution)/shard_map/ppermute | solution.py:14
  1.8 6.5 %collective-permute-start.1 = (f32[4,3,2304]{2,0,1:T(4,128)}, f32[4,3,2304]{2,0,1:T(4,128)S(1)}, u32[]{:S(2)}, u32[]{:S(2)}) collective-permute-start(f32[4,3,2304]{2,0,1:T(4,128)} %param.3), channel_id=1, source_target_pairs={{224,0},{240,16},{0,32},{16,48},{32,64},{48,80},{64,96},{80,112},{... | collective-permute-start | bytes 331784 | tf_op jit(solution)/shard_map/ppermute | solution.py:14
  3.0 6.6 %collective-permute-start.2 = (f32[4,3,2304]{2,0,1:T(4,128)}, f32[4,3,2304]{2,0,1:T(4,128)S(1)}, u32[]{:S(2)}, u32[]{:S(2)}) collective-permute-start(f32[4,3,2304]{2,0,1:T(4,128)} %param.3), channel_id=1, source_target_pairs={{208,0},{224,16},{240,32},{0,48},{16,64},{32,80},{48,96},{64,112},... | collective-permute-start | bytes 331784 | tf_op jit(solution)/shard_map/ppermute | solution.py:14
  4.2 7.0 %collective-permute-start.3 = (f32[4,3,2304]{2,0,1:T(4,128)}, f32[4,3,2304]{2,0,1:T(4,128)S(1)}, u32[]{:S(2)}, u32[]{:S(2)}) collective-permute-start(f32[4,3,2304]{2,0,1:T(4,128)} %param.3), channel_id=1, source_target_pairs={{192,0},{208,16},{224,32},{240,48},{0,64},{16,80},{32,96},{48,112}... | collective-permute-start | bytes 331784 | tf_op jit(solution)/shard_map/ppermute | solution.py:14
  6.6 7.1 %collective-permute-start.4 = (f32[4,3,2304]{2,0,1:T(4,128)}, f32[4,3,2304]{2,0,1:T(4,128)S(1)}, u32[]{:S(2)}, u32[]{:S(2)}) collective-permute-start(f32[4,3,2304]{2,0,1:T(4,128)} %param.3), channel_id=1, source_target_pairs={{176,0},{192,16},{208,32},{224,48},{240,64},{0,80},{16,96},{32,112... | collective-permute-start | bytes 331784 | tf_op jit(solution)/shard_map/ppermute | solution.py:14
  6.6 10.0 %collective-permute-start.5 = (f32[4,3,2304]{2,0,1:T(4,128)}, f32[4,3,2304]{2,0,1:T(4,128)S(1)}, u32[]{:S(2)}, u32[]{:S(2)}) collective-permute-start(f32[4,3,2304]{2,0,1:T(4,128)} %param.3), channel_id=1, source_target_pairs={{160,0},{176,16},{192,32},{208,48},{224,64},{240,80},{0,96},{16,11... | collective-permute-start | bytes 331784 | tf_op jit(solution)/shard_map/ppermute | solution.py:14
  8.3 8.8 %collective-permute-start.6 = (f32[4,3,2304]{2,0,1:T(4,128)}, f32[4,3,2304]{2,0,1:T(4,128)S(1)}, u32[]{:S(2)}, u32[]{:S(2)}) collective-permute-start(f32[4,3,2304]{2,0,1:T(4,128)} %param.3), channel_id=1, source_target_pairs={{144,0},{160,16},{176,32},{192,48},{208,64},{224,80},{240,96},{0,1... | collective-permute-start | bytes 331784 | tf_op jit(solution)/shard_map/ppermute | solution.py:14
  9.6 7.5 %collective-permute-start.7 = (f32[4,3,2304]{2,0,1:T(4,128)}, f32[4,3,2304]{2,0,1:T(4,128)S(1)}, u32[]{:S(2)}, u32[]{:S(2)}) collective-permute-start(f32[4,3,2304]{2,0,1:T(4,128)} %param.3), channel_id=1, source_target_pairs={{128,0},{144,16},{160,32},{176,48},{192,64},{208,80},{224,96},{240... | collective-permute-start | bytes 331784 | tf_op jit(solution)/shard_map/ppermute | solution.py:14
  19.7 2.3 copy-start
  22.0 131.5 %all-to-all-start = ((f32[16,9,3,2304]{3,2,1,0:T(4,128)}), f32[16,9,3,2304]{3,2,1,0:T(4,128)}, u32[]{:S(2)}, u32[]{:S(2)}) async-start(f32[16,9,3,2304]{3,2,1,0:T(4,128)} %bitcast.56), calls=%async_computation | async-start | bytes 10616832 | tf_op jit(solution)/shard_map/all_to_all | solution.py:62
  340.7 10.1 %copy-start.2 = (s32[4]{0:T(128)S(1)}, s32[4]{0:T(128)}, u32[]{:S(2)}) copy-start(s32[4]{0:T(128)} %param.4) | copy-start | bytes 52
  340.7 21.6 %copy-start.1 = (f32[4,3,2304]{2,0,1:T(4,128)S(1)}, f32[4,3,2304]{2,0,1:T(4,128)}, u32[]{:S(2)}) copy-start(f32[4,3,2304]{2,0,1:T(4,128)} %param.3) | copy-start | bytes 331780
  340.7 101.8 %all-to-all-start.1 = ((f32[1,9,48,2304]{3,0,1,2:T(1,128)}), f32[1,9,48,2304]{3,0,1,2:T(1,128)}, u32[]{:S(2)}, u32[]{:S(2)}) async-start(f32[1,9,48,2304]{3,0,1,2:T(1,128)} %copy.140), calls=%async_computation.1 | async-start | bytes 7962624 | tf_op jit(solution)/shard_map/all_to_all | solution.py:65
  350.8 11.7 %collective-permute-start.8 = (f32[4]{0:T(128)S(1)}, f32[4]{0:T(128)S(1)}, u32[]{:S(2)}, u32[]{:S(2)}) collective-permute-start(f32[4]{0:T(128)S(1)} %convert_multiply_fusion), channel_id=1, source_target_pairs={{240,0},{0,16},{16,32},{32,48},{48,64},{64,80},{80,96},{96,112},{1... | collective-permute-start | bytes 56 | tf_op jit(solution)/shard_map/ppermute | solution.py:14
  357.9 4.8 collective-permute-start.10
  357.9 7.9 %collective-permute-start.12 = (f32[4]{0:T(128)S(1)}, f32[4]{0:T(128)S(1)}, u32[]{:S(2)}, u32[]{:S(2)}) collective-permute-start(f32[4]{0:T(128)S(1)} %convert_multiply_fusion), channel_id=1, source_target_pairs={{208,0},{224,16},{240,32},{0,48},{16,64},{32,80},{48,96},{64,112},... | collective-permute-start | bytes 56 | tf_op jit(solution)/shard_map/ppermute | solution.py:14
  357.9 8.2 %collective-permute-start.14 = (f32[4]{0:T(128)S(1)}, f32[4]{0:T(128)S(1)}, u32[]{:S(2)}, u32[]{:S(2)}) collective-permute-start(f32[4]{0:T(128)S(1)} %convert_multiply_fusion), channel_id=1, source_target_pairs={{192,0},{208,16},{224,32},{240,48},{0,64},{16,80},{32,96},{48,112}... | collective-permute-start | bytes 56 | tf_op jit(solution)/shard_map/ppermute | solution.py:14
  362.3 4.9 %collective-permute-start.16 = (f32[4]{0:T(128)S(1)}, f32[4]{0:T(128)S(1)}, u32[]{:S(2)}, u32[]{:S(2)}) collective-permute-start(f32[4]{0:T(128)S(1)} %convert_multiply_fusion), channel_id=1, source_target_pairs={{176,0},{192,16},{208,32},{224,48},{240,64},{0,80},{16,96},{32,112... | collective-permute-start | bytes 56 | tf_op jit(solution)/shard_map/ppermute | solution.py:14
  362.5 4.9 %collective-permute-start.18 = (f32[4]{0:T(128)S(1)}, f32[4]{0:T(128)S(1)}, u32[]{:S(2)}, u32[]{:S(2)}) collective-permute-start(f32[4]{0:T(128)S(1)} %convert_multiply_fusion), channel_id=1, source_target_pairs={{160,0},{176,16},{192,32},{208,48},{224,64},{240,80},{0,96},{16,11... | collective-permute-start | bytes 56 | tf_op jit(solution)/shard_map/ppermute | solution.py:14
  362.7 5.1 %collective-permute-start.20 = (f32[4]{0:T(128)S(1)}, f32[4]{0:T(128)S(1)}, u32[]{:S(2)}, u32[]{:S(2)}) collective-permute-start(f32[4]{0:T(128)S(1)} %convert_multiply_fusion), channel_id=1, source_target_pairs={{144,0},{160,16},{176,32},{192,48},{208,64},{224,80},{240,96},{0,1... | collective-permute-start | bytes 56 | tf_op jit(solution)/shard_map/ppermute | solution.py:14
  365.8 92.4 %collective-permute-start.22 = (f32[4]{0:T(128)S(1)}, f32[4]{0:T(128)S(1)}, u32[]{:S(2)}, u32[]{:S(2)}) collective-permute-start(f32[4]{0:T(128)S(1)} %convert_multiply_fusion), channel_id=1, source_target_pairs={{128,0},{144,16},{160,32},{176,48},{192,64},{208,80},{224,96},{240... | collective-permute-start | bytes 56 | tf_op jit(solution)/shard_map/ppermute | solution.py:14
  453.2 11.3 %collective-permute-start.11 = (f32[4,3,2304]{2,1,0:T(4,128)S(1)}, f32[4,3,2304]{2,1,0:T(4,128)S(1)}, u32[]{:S(2)}, u32[]{:S(2)}) collective-permute-start(f32[4,3,2304]{2,1,0:T(4,128)S(1)} %get-tuple-element.40), channel_id=1, source_target_pairs={{32,0},{48,16},{64,32},{80,48},{96,64},{112,80},{128,96},{144,112}... | collective-permute-start | bytes 331784 | tf_op jit(solution)/shard_map/ppermute | solution.py:14
  453.3 18.4 %collective-permute-start.13 = (f32[4,3,2304]{2,1,0:T(4,128)S(1)}, f32[4,3,2304]{2,1,0:T(4,128)S(1)}, u32[]{:S(2)}, u32[]{:S(2)}) collective-permute-start(f32[4,3,2304]{2,1,0:T(4,128)S(1)} %get-tuple-element.29), channel_id=1, source_target_pairs={{48,0},{64,16},{80,32},{96,48},{112,64},{128,80},{144,96},{160,112... | collective-permute-start | bytes 331784 | tf_op jit(solution)/shard_map/ppermute | solution.py:14
  458.3 13.5 %collective-permute-start.15 = (f32[4,3,2304]{2,1,0:T(4,128)S(1)}, f32[4,3,2304]{2,1,0:T(4,128)S(1)}, u32[]{:S(2)}, u32[]{:S(2)}) collective-permute-start(f32[4,3,2304]{2,1,0:T(4,128)S(1)} %get-tuple-element.31), channel_id=1, source_target_pairs={{64,0},{80,16},{96,32},{112,48},{128,64},{144,80},{160,96},{176,11... | collective-permute-start | bytes 331784 | tf_op jit(solution)/shard_map/ppermute | solution.py:14
  462.3 9.5 %collective-permute-start.17 = (f32[4,3,2304]{2,1,0:T(4,128)S(1)}, f32[4,3,2304]{2,1,0:T(4,128)S(1)}, u32[]{:S(2)}, u32[]{:S(2)}) collective-permute-start(f32[4,3,2304]{2,1,0:T(4,128)S(1)} %get-tuple-element.33), channel_id=1, source_target_pairs={{80,0},{96,16},{112,32},{128,48},{144,64},{160,80},{176,96},{192,1... | collective-permute-start | bytes 331784 | tf_op jit(solution)/shard_map/ppermute | solution.py:14
  462.8 14.5 %collective-permute-start.19 = (f32[4,3,2304]{2,1,0:T(4,128)S(1)}, f32[4,3,2304]{2,1,0:T(4,128)S(1)}, u32[]{:S(2)}, u32[]{:S(2)}) collective-permute-start(f32[4,3,2304]{2,1,0:T(4,128)S(1)} %get-tuple-element.35), channel_id=1, source_target_pairs={{96,0},{112,16},{128,32},{144,48},{160,64},{176,80},{192,96},{208,... | collective-permute-start | bytes 331784 | tf_op jit(solution)/shard_map/ppermute | solution.py:14
  464.5 17.3 %collective-permute-start.21 = (f32[4,3,2304]{2,1,0:T(4,128)S(1)}, f32[4,3,2304]{2,1,0:T(4,128)S(1)}, u32[]{:S(2)}, u32[]{:S(2)}) collective-permute-start(f32[4,3,2304]{2,1,0:T(4,128)S(1)} %get-tuple-element.38), channel_id=1, source_target_pairs={{112,0},{128,16},{144,32},{160,48},{176,64},{192,80},{208,96},{224... | collective-permute-start | bytes 331784 | tf_op jit(solution)/shard_map/ppermute | solution.py:14
  471.6 10.2 %collective-permute-start.9 = (f32[4,3,2304]{2,1,0:T(4,128)S(1)}, f32[4,3,2304]{2,1,0:T(4,128)S(1)}, u32[]{:S(2)}, u32[]{:S(2)}) collective-permute-start(f32[4,3,2304]{2,1,0:T(4,128)S(1)} %get-tuple-element.6), channel_id=1, source_target_pairs={{16,0},{32,16},{48,32},{64,48},{80,64},{96,80},{112,96},{128,112},... | collective-permute-start | bytes 331784 | tf_op jit(solution)/shard_map/ppermute | solution.py:14
where the time goes:
time: 491 us; the launch traced here: 483 us
  waiting for transfers between devices  214 us (44%)
  local copies, waits for them, and re-layouts  131 us (27%)
  matrix products  72.2 us (15%)
  starting transfers between devices  59.4 us (12%)
  other arithmetic  5.73 us (1%)
    all_to_all x1, waiting for transfers between devices, solve_pairs(): lax.all_to_all(shaped, 'grid', split_axis=0, concat_axis=2, tiled=True)  118 us
    all_to_all x1, waiting for transfers between devices, solve_pairs(): lax.all_to_all(potential, 'grid', split_axis=2, concat_axis=0, tiled=True)  74.5 us
    dot_general x2, matrix products, apply_transform(): jnp.matmul(second.reshape(batch_size * extent * extent, extent), matrix.T...  40.5 us
    reshape x4, local copies, waits for them, and re-layouts, apply_transform(): first.reshape(batch_size * extent, extent, extent)  39.8 us
    ppermute x23, starting transfers between devices, shifted(): return lax.ppermute(block, axis, route)  39 us
    ppermute x23, waiting for transfers between devices, shifted(): return lax.ppermute(block, axis, route)  21.2 us
    reshape x2, local copies, waits for them, and re-layouts, apply_transform(): second.reshape(batch_size * extent * extent, extent)  18.4 us
    another operation x2, local copies, waits for them, and re-layouts, solve_pairs(): screened_potential(fields, transform, kernel).reshape(pieces.shape)  17.6 us
  transfers between devices with their start and end apart: 25, of which 10 were waited for; matrix products, arithmetic and copies ran while one was open for 3% of the time, Pallas kernels for 0%

commit v1 on v0

--- a/solution.py
+++ b/solution.py
@@ -59,7 +59,10 @@
     groups = lax.axis_size("grid")
     pair_count, planes, row_cells = densities.shape
     shaped = densities.reshape(groups, pair_count // groups, planes, row_cells)
-    pieces = lax.all_to_all(shaped, "grid", split_axis=0, concat_axis=2, tiled=True)
+    pieces = jnp.concatenate(
+        lax.all_to_all(jnp.stack(jnp.split(shaped, lax.axis_size("grid"), axis=0)), "grid", 0, 0),
+        axis=2,
+    )
     fields = pieces.reshape(pieces.shape[1], pieces.shape[2], pieces.shape[3])
     potential = screened_potential(fields, transform, kernel).reshape(pieces.shape)
     sliced = lax.all_to_all(potential, "grid", split_axis=2, concat_axis=0, tiled=True)

time: 491 us -> 474 us (0.965)
  waiting for transfers between devices: 214 us -> 183 us
  local copies, waits for them, and re-layouts: 131 us -> 142 us
    all_to_all x1, waiting for transfers between devices: 118 us -> 89.1 us  [solve_pairs(): lax.all_to_all(jnp.stack(jnp.split(shaped, lax.axis_size('grid'), axis=0)...]
    unnamed x15 -> x20, local copies, waits for them, and re-layouts: 4.41 us -> 15.3 us
    another operation x0 -> x7, local copies, waits for them, and re-layouts: none -> 7.97 us  [the longest x1 6.81 us: solve_pairs(): fields = pieces.reshape(pieces.shape[1], pieces.shape[2], pieces.shape[3])]
    all_to_all x1 -> x0, local copies, waits for them, and re-layouts: 5.91 us -> none  [solve_pairs(): lax.all_to_all(shaped, 'grid', split_axis=0, concat_axis=2, tiled=True)]
where the time goes in v1:
time: 474 us; the launch traced here: 467 us
  waiting for transfers between devices  183 us (39%)
  local copies, waits for them, and re-layouts  142 us (30%)
  matrix products  72.4 us (15%)
  starting transfers between devices  61.1 us (13%)
  other arithmetic  6.51 us (1%)
    all_to_all x1, waiting for transfers between devices, solve_pairs(): lax.all_to_all(jnp.stack(jnp.split(shaped, lax.axis_size('grid'), axis=0)...  89.1 us
    all_to_all x1, waiting for transfers between devices, solve_pairs(): lax.all_to_all(potential, 'grid', split_axis=2, concat_axis=0, tiled=True)  73.6 us
    dot_general x2, matrix products, apply_transform(): jnp.matmul(second.reshape(batch_size * extent * extent, extent), matrix.T...  40.5 us
    ppermute x23, starting transfers between devices, shifted(): return lax.ppermute(block, axis, route)  40 us
    reshape x4, local copies, waits for them, and re-layouts, apply_transform(): first.reshape(batch_size * extent, extent, extent)  39.5 us
    ppermute x23, waiting for transfers between devices, shifted(): return lax.ppermute(block, axis, route)  20.7 us
    reshape x2, local copies, waits for them, and re-layouts, apply_transform(): second.reshape(batch_size * extent * extent, extent)  18.2 us
    another operation x2, local copies, waits for them, and re-layouts, solve_pairs(): screened_potential(fields, transform, kernel).reshape(pieces.shape)  17.6 us
  transfers between devices with their start and end apart: 25, of which 10 were waited for; matrix products, arithmetic and copies ran while one was open for 3% of the time, Pallas kernels for 0%

profile of v1, /device:TPU:7, one launch (start us, length us, event | category | flops | bytes accessed | tf_op | source)
XLA Modules:
  0.0 467.2 jit_solution(16686790904590908080)
XLA Ops:
  0.0 1.8 collective-permute-start
  1.8 1.2 collective-permute-start.1
  3.0 1.2 collective-permute-start.2
  4.2 2.4 collective-permute-start.3
  6.6 1.7 collective-permute-start.5
  8.3 1.2 collective-permute-start.6
  9.6 1.0 collective-permute-start.7
  10.5 1.0 copy.179
  11.7 2.0 collective-permute-done.4
  13.7 2.9 collective-permute-done.5
  17.2 1.2 broadcast_multiply_fusion
  34.7 10.4 %all-to-all-start = ((f32[16,1,9,3,2304]{4,1,3,2,0:T(1,128)}), f32[16,1,9,3,2304]{4,1,3,2,0:T(1,128)}, u32[]{:S(2)}, u32[]{:S(2)}) async-start(f32[16,1,9,3,2304]{4,1,3,2,0:T(1,128)} %reshape_dynamic-update-slice_fusion), calls=%async_computation | async-start | bytes 7962624 | tf_op jit(solution)/shard_map/all_to_all | solution.py:63
  48.2 89.1 %all-to-all-done = f32[16,1,9,3,2304]{4,1,3,2,0:T(1,128)} async-done(((f32[16,1,9,3,2304]{4,1,3,2,0:T(1,128)}), f32[16,1,9,3,2304]{4,1,3,2,0:T(1,128)}, u32[]{:S(2)}, u32[]{:S(2)}) %all-to-all-start) | async-done | bytes 3981344 | tf_op jit(solution)/shard_map/all_to_all | solution.py:63
  137.2 5.8 %copy.204 = f32[1,9,16,3,2304]{4,3,2,1,0:T(4,128)} copy(f32[1,9,16,3,2304]{4,0,3,1,2:T(1,128)} %bitcast.27) | data formatting | bytes 7962624 | tf_op jit(solution)/shard_map/reshape | solution.py:62
  143.0 6.8 %reshape_reshape.9 = f32[9,48,2304]{2,1,0:T(8,128)} reshape(f32[1,9,16,3,2304]{4,3,2,1,0:T(4,128)} %copy.204) | data formatting | bytes 7962624 | tf_op jit(solution)/shard_map/reshape;reshape | solution.py:66
  149.9 7.7 %convolution_bitcast_fusion.1 = f32[9,48,2304]{2,1,0:T(8,128)} fusion(f32[9,48,2304]{2,1,0:T(8,128)} %reshape_reshape.9, s32[48]{0:T(128)S(1)} %add_select_fusion.1, pred[48]{0:T(512)(128)(4,1)S(1)} %iota_compare_fusion), kind=kOutput, calls=%fused_computation.1 | convolution fusion | flops 573331968 | bytes 7962864 | tf_op jit(solution)/shard_map/dot_general | solution.py:41
  157.6 10.3 %reshape.363 = f32[432,48,48]{2,1,0:T(8,128)} reshape(f32[9,48,2304]{2,1,0:T(8,128)} %convolution_bitcast_fusion.1) | data formatting | bytes 7962624 | tf_op jit(solution)/shard_map/reshape | solution.py:43
  167.8 9.5 %copy.207 = f32[432,48,48]{0,1,2:T(8,128)} copy(f32[432,48,48]{2,1,0:T(8,128)} %reshape.363) | data formatting | bytes 7962624 | tf_op jit(solution)/shard_map/reshape | solution.py:43
  177.3 7.9 %convolution_bitcast_fusion.3 = f32[432,48,48]{0,1,2:T(8,128)} fusion(f32[432,48,48]{0,1,2:T(8,128)} %copy.207, s32[48]{0:T(128)S(1)} %add_select_fusion.1, pred[48]{0:T(512)(128)(4,1)S(1)} %iota_compare_fusion), kind=kOutput, calls=%fused_computation.4 | convolution fusion | flops 573331968 | bytes 7962864 | tf_op jit(solution)/shard_map/dot_general | solution.py:42
  185.1 8.5 %copy.208 = f32[432,48,48]{1,0,2:T(8,128)} copy(f32[432,48,48]{0,1,2:T(8,128)} %convolution_bitcast_fusion.3) | data formatting | bytes 7962624 | tf_op jit(solution)/shard_map/transpose | solution.py:42
  193.6 9.1 %reshape.364 = f32[20736,48]{0,1:T(8,128)} reshape(f32[432,48,48]{1,0,2:T(8,128)} %copy.208) | data formatting | bytes 7962624 | tf_op jit(solution)/shard_map/reshape | solution.py:46
  202.7 20.2 %fusion.19 = f32[20736,48]{1,0:T(8,128)} fusion(f32[20736,48]{0,1:T(8,128)} %reshape.364, s32[48]{0:T(128)S(1)} %add_select_fusion.1, pred[48]{0:T(512)(128)(4,1)S(1)} %iota_compare_fusion), kind=kOutput, calls=%fused_computation.95 | convolution fusion | flops 573331968 | bytes 7962864 | tf_op jit(solution)/shard_map/dot_general | solution.py:45
  222.9 10.0 %reshape.365 = f32[9,48,2304]{2,1,0:T(8,128)} reshape(f32[20736,48]{1,0:T(8,128)} %fusion.19) | data formatting | bytes 7962624 | tf_op jit(solution)/shard_map/reshape | solution.py:50
  232.9 7.7 %convolution_bitcast_fusion = f32[9,48,2304]{2,1,0:T(8,128)} fusion(f32[9,48,2304]{2,1,0:T(8,128)} %reshape.365, f32[48,2304]{1,0:T(8,128)S(1)} %multiply_select_fusion, s32[48]{0:T(128)S(1)} %add_select_fusion.1, pred[48]{0:T(512)(128)(4,1)S(1)} %iota_compare_fusion), kind=kOutput, calls=%fused_computation | convolution fusion | flops 574327296 | bytes 8405232 | tf_op jit(solution)/shard_map/dot_general | solution.py:41
  240.5 10.3 %reshape.366 = f32[432,48,48]{2,1,0:T(8,128)} reshape(f32[9,48,2304]{2,1,0:T(8,128)} %convolution_bitcast_fusion) | data formatting | bytes 7962624 | tf_op jit(solution)/shard_map/reshape | solution.py:43
  250.8 9.5 %copy.210 = f32[432,48,48]{0,1,2:T(8,128)} copy(f32[432,48,48]{2,1,0:T(8,128)} %reshape.366) | data formatting | bytes 7962624 | tf_op jit(solution)/shard_map/reshape | solution.py:43
  260.3 8.6 %convolution_bitcast_fusion.2 = f32[432,48,48]{0,1,2:T(8,128)} fusion(f32[432,48,48]{0,1,2:T(8,128)} %copy.210, s32[48]{0:T(128)S(1)} %add_select_fusion.1, pred[48]{0:T(512)(128)(4,1)S(1)} %iota_compare_fusion), kind=kOutput, calls=%fused_computation.3 | convolution fusion | flops 573331968 | bytes 7962864 | tf_op jit(solution)/shard_map/dot_general | solution.py:42
  268.9 8.5 %copy.211 = f32[432,48,48]{1,0,2:T(8,128)} copy(f32[432,48,48]{0,1,2:T(8,128)} %convolution_bitcast_fusion.2) | data formatting | bytes 7962624 | tf_op jit(solution)/shard_map/transpose | solution.py:42
  277.4 9.1 %reshape.367 = f32[20736,48]{0,1:T(8,128)} reshape(f32[432,48,48]{1,0,2:T(8,128)} %copy.211) | data formatting | bytes 7962624 | tf_op jit(solution)/shard_map/reshape | solution.py:46
  286.5 20.3 %fusion.20 = f32[20736,48]{1,0:T(8,128)} fusion(f32[20736,48]{0,1:T(8,128)} %reshape.367, s32[48]{0:T(128)S(1)} %add_select_fusion.1, pred[48]{0:T(512)(128)(4,1)S(1)} %iota_compare_fusion), kind=kOutput, calls=%fused_computation.96 | convolution fusion | flops 573331968 | bytes 7962864 | tf_op jit(solution)/shard_map/dot_general | solution.py:45
  306.8 9.5 %reshape_reshape.10 = f32[1,9,48,2304]{3,2,1,0:T(8,128)} reshape(f32[20736,48]{1,0:T(8,128)} %fusion.20) | data formatting | bytes 7962624 | tf_op jit(solution)/shard_map/reshape;reshape | solution.py:67
  316.3 8.1 %copy.213 = f32[1,9,48,2304]{3,0,1,2:T(1,128)} copy(f32[1,9,48,2304]{3,2,1,0:T(8,128)} %reshape_reshape.10) | data formatting | bytes 7962624 | tf_op jit(solution)/shard_map/reshape;reshape | solution.py:67
  324.4 10.7 %all-to-all-start.1 = ((f32[1,9,48,2304]{3,0,1,2:T(1,128)}), f32[1,9,48,2304]{3,0,1,2:T(1,128)}, u32[]{:S(2)}, u32[]{:S(2)}) async-start(f32[1,9,48,2304]{3,0,1,2:T(1,128)} %copy.213), calls=%async_computation.1 | async-start | bytes 7962624 | tf_op jit(solution)/shard_map/all_to_all | solution.py:68
  335.1 6.4 %collective-permute-start.8 = (f32[4]{0:T(128)S(1)}, f32[4]{0:T(128)S(1)}, u32[]{:S(2)}, u32[]{:S(2)}) collective-permute-start(f32[4]{0:T(128)S(1)} %convert_multiply_fusion), channel_id=1, source_target_pairs={{240,0},{0,16},{16,32},{32,48},{48,64},{64,80},{80,96},{96,112},{1... | collective-permute-start | bytes 56 | tf_op jit(solution)/shard_map/ppermute | solution.py:14
  341.6 4.4 collective-permute-start.14
  346.4 2.9 collective-permute-start.20
  351.7 73.6 %all-to-all-done.1 = f32[1,9,48,2304]{3,0,1,2:T(1,128)} async-done(((f32[1,9,48,2304]{3,0,1,2:T(1,128)}), f32[1,9,48,2304]{3,0,1,2:T(1,128)}, u32[]{:S(2)}, u32[]{:S(2)}) %all-to-all-start.1) | async-done | bytes 3981344 | tf_op jit(solution)/shard_map/all_to_all | solution.py:68
  425.3 5.3 %copy.214 = f32[1,9,48,2304]{3,0,2,1:T(1,128)S(1)} copy(f32[1,9,48,2304]{3,0,1,2:T(1,128)} %all-to-all-done.1) | data formatting | bytes 7962624 | tf_op jit(solution)/shard_map/all_to_all | solution.py:68
  430.6 1.4 copy.215
  431.9 1.1 fusion.40
  433.1 2.9 multiply_reduce_fusion.14
  436.0 6.6 %collective-permute-start.13 = (f32[4,3,2304]{2,1,0:T(4,128)S(1)}, f32[4,3,2304]{2,1,0:T(4,128)S(1)}, u32[]{:S(2)}, u32[]{:S(2)}) collective-permute-start(f32[4,3,2304]{2,1,0:T(4,128)S(1)} %get-tuple-element.40), channel_id=1, source_target_pairs={{48,0},{64,16},{80,32},{96,48},{112,64},{128,80},{144,96},{160,112... | collective-permute-start | bytes 331784 | tf_op jit(solution)/shard_map/ppermute | solution.py:14
  442.8 3.4 collective-permute-start.15
  446.1 2.0 collective-permute-start.17
  448.2 3.2 collective-permute-start.21
  451.4 4.0 collective-permute-done.13
  455.5 6.0 %collective-permute-done.19 = f32[4,3,2304]{2,1,0:T(4,128)S(1)} collective-permute-done((f32[4,3,2304]{2,1,0:T(4,128)S(1)}, f32[4,3,2304]{2,1,0:T(4,128)S(1)}, u32[]{:S(2)}, u32[]{:S(2)}) %collective-permute-start.19) | collective-permute-done | bytes 110624 | tf_op jit(solution)/shard_map/ppermute | solution.py:14
  461.5 4.3 collective-permute-done.21
  (98 shorter events, 23.4 us)
Async XLA Ops:
  0.0 6.6 %collective-permute-start = (f32[4,3,2304]{2,0,1:T(4,128)}, f32[4,3,2304]{2,0,1:T(4,128)S(1)}, u32[]{:S(2)}, u32[]{:S(2)}) collective-permute-start(f32[4,3,2304]{2,0,1:T(4,128)} %param.3), channel_id=1, source_target_pairs={{240,0},{0,16},{16,32},{32,48},{48,64},{64,80},{80,96},{96,112},{1... | collective-permute-start | bytes 331784 | tf_op jit(solution)/shard_map/ppermute | solution.py:14
  1.8 6.5 %collective-permute-start.1 = (f32[4,3,2304]{2,0,1:T(4,128)}, f32[4,3,2304]{2,0,1:T(4,128)S(1)}, u32[]{:S(2)}, u32[]{:S(2)}) collective-permute-start(f32[4,3,2304]{2,0,1:T(4,128)} %param.3), channel_id=1, source_target_pairs={{224,0},{240,16},{0,32},{16,48},{32,64},{48,80},{64,96},{80,112},{... | collective-permute-start | bytes 331784 | tf_op jit(solution)/shard_map/ppermute | solution.py:14
  3.0 6.6 %collective-permute-start.2 = (f32[4,3,2304]{2,0,1:T(4,128)}, f32[4,3,2304]{2,0,1:T(4,128)S(1)}, u32[]{:S(2)}, u32[]{:S(2)}) collective-permute-start(f32[4,3,2304]{2,0,1:T(4,128)} %param.3), channel_id=1, source_target_pairs={{208,0},{224,16},{240,32},{0,48},{16,64},{32,80},{48,96},{64,112},... | collective-permute-start | bytes 331784 | tf_op jit(solution)/shard_map/ppermute | solution.py:14
  4.2 7.5 %collective-permute-start.3 = (f32[4,3,2304]{2,0,1:T(4,128)}, f32[4,3,2304]{2,0,1:T(4,128)S(1)}, u32[]{:S(2)}, u32[]{:S(2)}) collective-permute-start(f32[4,3,2304]{2,0,1:T(4,128)} %param.3), channel_id=1, source_target_pairs={{192,0},{208,16},{224,32},{240,48},{0,64},{16,80},{32,96},{48,112}... | collective-permute-start | bytes 331784 | tf_op jit(solution)/shard_map/ppermute | solution.py:14
  6.6 7.1 %collective-permute-start.4 = (f32[4,3,2304]{2,0,1:T(4,128)}, f32[4,3,2304]{2,0,1:T(4,128)S(1)}, u32[]{:S(2)}, u32[]{:S(2)}) collective-permute-start(f32[4,3,2304]{2,0,1:T(4,128)} %param.3), channel_id=1, source_target_pairs={{176,0},{192,16},{208,32},{224,48},{240,64},{0,80},{16,96},{32,112... | collective-permute-start | bytes 331784 | tf_op jit(solution)/shard_map/ppermute | solution.py:14
  6.6 10.0 %collective-permute-start.5 = (f32[4,3,2304]{2,0,1:T(4,128)}, f32[4,3,2304]{2,0,1:T(4,128)S(1)}, u32[]{:S(2)}, u32[]{:S(2)}) collective-permute-start(f32[4,3,2304]{2,0,1:T(4,128)} %param.3), channel_id=1, source_target_pairs={{160,0},{176,16},{192,32},{208,48},{224,64},{240,80},{0,96},{16,11... | collective-permute-start | bytes 331784 | tf_op jit(solution)/shard_map/ppermute | solution.py:14
  8.3 8.8 %collective-permute-start.6 = (f32[4,3,2304]{2,0,1:T(4,128)}, f32[4,3,2304]{2,0,1:T(4,128)S(1)}, u32[]{:S(2)}, u32[]{:S(2)}) collective-permute-start(f32[4,3,2304]{2,0,1:T(4,128)} %param.3), channel_id=1, source_target_pairs={{144,0},{160,16},{176,32},{192,48},{208,64},{224,80},{240,96},{0,1... | collective-permute-start | bytes 331784 | tf_op jit(solution)/shard_map/ppermute | solution.py:14
  9.6 7.5 %collective-permute-start.7 = (f32[4,3,2304]{2,0,1:T(4,128)}, f32[4,3,2304]{2,0,1:T(4,128)S(1)}, u32[]{:S(2)}, u32[]{:S(2)}) collective-permute-start(f32[4,3,2304]{2,0,1:T(4,128)} %param.3), channel_id=1, source_target_pairs={{128,0},{144,16},{160,32},{176,48},{192,64},{208,80},{224,96},{240... | collective-permute-start | bytes 331784 | tf_op jit(solution)/shard_map/ppermute | solution.py:14
  34.7 102.6 %all-to-all-start = ((f32[16,1,9,3,2304]{4,1,3,2,0:T(1,128)}), f32[16,1,9,3,2304]{4,1,3,2,0:T(1,128)}, u32[]{:S(2)}, u32[]{:S(2)}) async-start(f32[16,1,9,3,2304]{4,1,3,2,0:T(1,128)} %reshape_dynamic-update-slice_fusion), calls=%async_computation | async-start | bytes 7962624 | tf_op jit(solution)/shard_map/all_to_all | solution.py:63
  324.4 10.7 %copy-start.1 = (s32[4]{0:T(128)S(1)}, s32[4]{0:T(128)}, u32[]{:S(2)}) copy-start(s32[4]{0:T(128)} %param.4) | copy-start | bytes 52
  324.4 21.6 %copy-start = (f32[4,3,2304]{2,0,1:T(4,128)S(1)}, f32[4,3,2304]{2,0,1:T(4,128)}, u32[]{:S(2)}) copy-start(f32[4,3,2304]{2,0,1:T(4,128)} %param.3) | copy-start | bytes 331780
  324.4 100.8 %all-to-all-start.1 = ((f32[1,9,48,2304]{3,0,1,2:T(1,128)}), f32[1,9,48,2304]{3,0,1,2:T(1,128)}, u32[]{:S(2)}, u32[]{:S(2)}) async-start(f32[1,9,48,2304]{3,0,1,2:T(1,128)} %copy.213), calls=%async_computation.1 | async-start | bytes 7962624 | tf_op jit(solution)/shard_map/all_to_all | solution.py:68
  335.1 11.0 %collective-permute-start.8 = (f32[4]{0:T(128)S(1)}, f32[4]{0:T(128)S(1)}, u32[]{:S(2)}, u32[]{:S(2)}) collective-permute-start(f32[4]{0:T(128)S(1)} %convert_multiply_fusion), channel_id=1, source_target_pairs={{240,0},{0,16},{16,32},{32,48},{48,64},{64,80},{80,96},{96,112},{1... | collective-permute-start | bytes 56 | tf_op jit(solution)/shard_map/ppermute | solution.py:14
  341.6 4.8 %collective-permute-start.10 = (f32[4]{0:T(128)S(1)}, f32[4]{0:T(128)S(1)}, u32[]{:S(2)}, u32[]{:S(2)}) collective-permute-start(f32[4]{0:T(128)S(1)} %convert_multiply_fusion), channel_id=1, source_target_pairs={{224,0},{240,16},{0,32},{16,48},{32,64},{48,80},{64,96},{80,112},{... | collective-permute-start | bytes 56 | tf_op jit(solution)/shard_map/ppermute | solution.py:14
  341.6 7.9 %collective-permute-start.12 = (f32[4]{0:T(128)S(1)}, f32[4]{0:T(128)S(1)}, u32[]{:S(2)}, u32[]{:S(2)}) collective-permute-start(f32[4]{0:T(128)S(1)} %convert_multiply_fusion), channel_id=1, source_target_pairs={{208,0},{224,16},{240,32},{0,48},{16,64},{32,80},{48,96},{64,112},... | collective-permute-start | bytes 56 | tf_op jit(solution)/shard_map/ppermute | solution.py:14
  341.6 8.4 %collective-permute-start.14 = (f32[4]{0:T(128)S(1)}, f32[4]{0:T(128)S(1)}, u32[]{:S(2)}, u32[]{:S(2)}) collective-permute-start(f32[4]{0:T(128)S(1)} %convert_multiply_fusion), channel_id=1, source_target_pairs={{192,0},{208,16},{224,32},{240,48},{0,64},{16,80},{32,96},{48,112}... | collective-permute-start | bytes 56 | tf_op jit(solution)/shard_map/ppermute | solution.py:14
  346.0 4.9 %collective-permute-start.16 = (f32[4]{0:T(128)S(1)}, f32[4]{0:T(128)S(1)}, u32[]{:S(2)}, u32[]{:S(2)}) collective-permute-start(f32[4]{0:T(128)S(1)} %convert_multiply_fusion), channel_id=1, source_target_pairs={{176,0},{192,16},{208,32},{224,48},{240,64},{0,80},{16,96},{32,112... | collective-permute-start | bytes 56 | tf_op jit(solution)/shard_map/ppermute | solution.py:14
  346.2 4.9 %collective-permute-start.18 = (f32[4]{0:T(128)S(1)}, f32[4]{0:T(128)S(1)}, u32[]{:S(2)}, u32[]{:S(2)}) collective-permute-start(f32[4]{0:T(128)S(1)} %convert_multiply_fusion), channel_id=1, source_target_pairs={{160,0},{176,16},{192,32},{208,48},{224,64},{240,80},{0,96},{16,11... | collective-permute-start | bytes 56 | tf_op jit(solution)/shard_map/ppermute | solution.py:14
  346.4 5.1 %collective-permute-start.20 = (f32[4]{0:T(128)S(1)}, f32[4]{0:T(128)S(1)}, u32[]{:S(2)}, u32[]{:S(2)}) collective-permute-start(f32[4]{0:T(128)S(1)} %convert_multiply_fusion), channel_id=1, source_target_pairs={{144,0},{160,16},{176,32},{192,48},{208,64},{224,80},{240,96},{0,1... | collective-permute-start | bytes 56 | tf_op jit(solution)/shard_map/ppermute | solution.py:14
  349.5 93.2 %collective-permute-start.22 = (f32[4]{0:T(128)S(1)}, f32[4]{0:T(128)S(1)}, u32[]{:S(2)}, u32[]{:S(2)}) collective-permute-start(f32[4]{0:T(128)S(1)} %convert_multiply_fusion), channel_id=1, source_target_pairs={{128,0},{144,16},{160,32},{176,48},{192,64},{208,80},{224,96},{240... | collective-permute-start | bytes 56 | tf_op jit(solution)/shard_map/ppermute | solution.py:14
  435.9 12.3 %collective-permute-start.11 = (f32[4,3,2304]{2,1,0:T(4,128)S(1)}, f32[4,3,2304]{2,1,0:T(4,128)S(1)}, u32[]{:S(2)}, u32[]{:S(2)}) collective-permute-start(f32[4,3,2304]{2,1,0:T(4,128)S(1)} %get-tuple-element.51), channel_id=1, source_target_pairs={{32,0},{48,16},{64,32},{80,48},{96,64},{112,80},{128,96},{144,112}... | collective-permute-start | bytes 331784 | tf_op jit(solution)/shard_map/ppermute | solution.py:14
  436.0 19.3 %collective-permute-start.13 = (f32[4,3,2304]{2,1,0:T(4,128)S(1)}, f32[4,3,2304]{2,1,0:T(4,128)S(1)}, u32[]{:S(2)}, u32[]{:S(2)}) collective-permute-start(f32[4,3,2304]{2,1,0:T(4,128)S(1)} %get-tuple-element.40), channel_id=1, source_target_pairs={{48,0},{64,16},{80,32},{96,48},{112,64},{128,80},{144,96},{160,112... | collective-permute-start | bytes 331784 | tf_op jit(solution)/shard_map/ppermute | solution.py:14
  442.8 12.7 %collective-permute-start.15 = (f32[4,3,2304]{2,1,0:T(4,128)S(1)}, f32[4,3,2304]{2,1,0:T(4,128)S(1)}, u32[]{:S(2)}, u32[]{:S(2)}) collective-permute-start(f32[4,3,2304]{2,1,0:T(4,128)S(1)} %get-tuple-element.42), channel_id=1, source_target_pairs={{64,0},{80,16},{96,32},{112,48},{128,64},{144,80},{160,96},{176,11... | collective-permute-start | bytes 331784 | tf_op jit(solution)/shard_map/ppermute | solution.py:14
  446.1 9.4 %collective-permute-start.17 = (f32[4,3,2304]{2,1,0:T(4,128)S(1)}, f32[4,3,2304]{2,1,0:T(4,128)S(1)}, u32[]{:S(2)}, u32[]{:S(2)}) collective-permute-start(f32[4,3,2304]{2,1,0:T(4,128)S(1)} %get-tuple-element.44), channel_id=1, source_target_pairs={{80,0},{96,16},{112,32},{128,48},{144,64},{160,80},{176,96},{192,1... | collective-permute-start | bytes 331784 | tf_op jit(solution)/shard_map/ppermute | solution.py:14
  448.1 13.4 %collective-permute-start.19 = (f32[4,3,2304]{2,1,0:T(4,128)S(1)}, f32[4,3,2304]{2,1,0:T(4,128)S(1)}, u32[]{:S(2)}, u32[]{:S(2)}) collective-permute-start(f32[4,3,2304]{2,1,0:T(4,128)S(1)} %get-tuple-element.46), channel_id=1, source_target_pairs={{96,0},{112,16},{128,32},{144,48},{160,64},{176,80},{192,96},{208,... | collective-permute-start | bytes 331784 | tf_op jit(solution)/shard_map/ppermute | solution.py:14
  448.2 17.6 %collective-permute-start.21 = (f32[4,3,2304]{2,1,0:T(4,128)S(1)}, f32[4,3,2304]{2,1,0:T(4,128)S(1)}, u32[]{:S(2)}, u32[]{:S(2)}) collective-permute-start(f32[4,3,2304]{2,1,0:T(4,128)S(1)} %get-tuple-element.49), channel_id=1, source_target_pairs={{112,0},{128,16},{144,32},{160,48},{176,64},{192,80},{208,96},{224... | collective-permute-start | bytes 331784 | tf_op jit(solution)/shard_map/ppermute | solution.py:14
  455.3 10.5 %collective-permute-start.9 = (f32[4,3,2304]{2,1,0:T(4,128)S(1)}, f32[4,3,2304]{2,1,0:T(4,128)S(1)}, u32[]{:S(2)}, u32[]{:S(2)}) collective-permute-start(f32[4,3,2304]{2,1,0:T(4,128)S(1)} %get-tuple-element.6), channel_id=1, source_target_pairs={{16,0},{32,16},{48,32},{64,48},{80,64},{96,80},{112,96},{128,112},... | collective-permute-start | bytes 331784 | tf_op jit(solution)/shard_map/ppermute | solution.py:14
